TPU v7x, 32 devices: a whole 2x2x4 slice. The times are simulated.
32 devices in a mesh: dp: 8 (over y, x, core), mp: 4 (over z).
Axes of the slice: x: 2, y: 2, z: 4, core: 2. Of those that a mesh axis runs over, the one named last changes fastest.
Arguments:
- hidden: bfloat16 [12288, 1024], P(('dp', 'mp')), may hold values from -6 to 6
- lengths: int32 [8], P('dp'), may hold values from 1 to 1536, 7372 in all
- first_gain: float32 [1024], replicated, may hold values from 0.5 to 1.5
- first_shift: float32 [1024], replicated, may hold values from -1.75 to 1.75
- projection_in: bfloat16 [1024, 3, 1024], P(None, None, 'mp'), may hold values from -0.1875 to 0.1875
- query_value_bias: float32 [2, 1024], P(None, 'mp'), may hold values from -0.625 to 0.625
- projection_out: bfloat16 [1024, 1024], P('mp'), may hold values from -2 to 2
- out_bias: float32 [1024], replicated, may hold values from -1.75 to 1.75
- second_gain: float32 [1024], replicated, may hold values from 0.5 to 1.5
- second_shift: float32 [1024], replicated, may hold values from -1.75 to 1.75
- up_weight: bfloat16 [1024, 4096], P(None, 'mp'), may hold values from -0.1875 to 0.1875
- up_bias: bfloat16 [4096], P('mp'), may hold values from -1.75 to 1.75
- down_weight: bfloat16 [4096, 1024], P('mp'), may hold values from -0.09375 to 0.09375
- down_bias: float32 [1024], replicated, may hold values from -1.75 to 1.75
- cotangent: bfloat16 [12288, 1024], P(('dp', 'mp')), may hold values from -6 to 6
Outputs:
- output: bfloat16 [12288, 1024], P(('dp', 'mp'))
- gradient_hidden: bfloat16 [12288, 1024], P(('dp', 'mp'))
- gradient_first_gain: float32 [1024], replicated
- gradient_first_shift: float32 [1024], replicated
- gradient_projection_in: float32 [1024, 3, 1024], P('dp', None, 'mp')
- gradient_query_value_bias: float32 [2, 1024], replicated
- gradient_projection_out: float32 [1024, 1024], P('mp', 'dp')
- gradient_out_bias: float32 [1024], replicated
- gradient_second_gain: float32 [1024], replicated
- gradient_second_shift: float32 [1024], replicated
- gradient_up_weight: float32 [1024, 4096], P('dp', 'mp')
- gradient_up_bias: float32 [4096], replicated
- gradient_down_weight: float32 [4096, 1024], P('mp', 'dp')
- gradient_down_bias: float32 [1024], replicated
Inputs may be any that keep to these rules, and one draw needn't show every extreme that they name: `lengths`: each utterance has at least one frame and at most 1536; the longest has exactly 1536.
All inputs are finite; a program needn't handle non-finite values. No bound on the sum of `lengths` on one device may be relied on, other than what follows from the above.
Results may differ from a plain program's by a relative error of at most 0.019.
Values may be sent and summed in bfloat16 or wider, within the bound.
No kernel may reach another device: no remote copies, remote signals or barrier semaphores. Data moves between devices by JAX's collectives and lax.ppermute only.
A program may use at most 128 MiB of HBM per device.

v0:
```python
import jax
import jax.numpy as jnp
from jax import lax
from jax.sharding import PartitionSpec as P

HEAD_DIM = 64
BLOCK = 512


EPS = 1e-05
NEGATIVE = -1e30


def normalize(values):
    centered = values - jnp.mean(values, -1, keepdims=True)
    inverse = lax.rsqrt(jnp.mean(centered * centered, -1, keepdims=True) + EPS)
    return (centered * inverse, inverse)


def norm_back(incoming, scaled_in, inverse, gain):
    weighted = incoming * gain
    return inverse * (
        weighted
        - jnp.mean(weighted, -1, keepdims=True)
        - scaled_in * jnp.mean(weighted * scaled_in, -1, keepdims=True)
    )


def over_rows(left, right):
    return lax.dot_general(
        left, right, (((0,), (0,)), ((), ())), preferred_element_type=jnp.float32
    )


def over_cols(left, right):
    return lax.dot_general(
        left, right, (((1,), (1,)), ((), ())), preferred_element_type=jnp.float32
    )


def exact_gelu(values):
    return jax.nn.gelu(values, approximate=False)


def split_heads(values):
    return values.reshape(values.shape[0], -1, HEAD_DIM)


def block_scores(query_heads, key_heads, start, length):
    query_block = lax.dynamic_slice_in_dim(query_heads, start, BLOCK, 0)
    scores = jnp.einsum("qhd,khd->hqk", query_block, key_heads, preferred_element_type=jnp.float32)
    positions = jnp.arange(key_heads.shape[0], dtype=jnp.int32)
    row_at = start + jnp.arange(BLOCK, dtype=jnp.int32)
    allowed = (positions[None, :] <= row_at[:, None]) & (positions[None, :] < length)
    return (query_block, jnp.where(allowed[None], scores, NEGATIVE))


def attend(queries, keys_in, values_in, length):
    seq_len = queries.shape[0]
    query_heads = split_heads(queries)
    key_heads = split_heads(keys_in)
    value_heads = split_heads(values_in)

    def forward_block(start):
        query_block, scores = block_scores(query_heads, key_heads, start, length)
        highest = jnp.max(scores, -1, keepdims=True)
        log_total = highest + jnp.log(jnp.sum(jnp.exp(scores - highest), -1, keepdims=True))
        weights = jnp.exp(scores - log_total).astype(jnp.bfloat16)
        context = jnp.einsum(
            "hqk,khd->qhd", weights, value_heads, preferred_element_type=jnp.float32
        )
        return (context.astype(jnp.bfloat16).reshape(BLOCK, -1), log_total[..., 0])

    starts = jnp.arange(seq_len // BLOCK, dtype=jnp.int32) * BLOCK
    context, log_total = lax.map(forward_block, starts)
    return (context.reshape(seq_len, -1), log_total)


def attend_back(queries, keys_in, values_in, back_context, log_total, length):
    seq_len = queries.shape[0]
    query_heads = split_heads(queries)
    key_heads = split_heads(keys_in)
    value_heads = split_heads(values_in)
    back_heads = split_heads(back_context)

    def back_block(carry, inputs):
        key_sum, value_sum = carry
        start, block_total = inputs
        query_block, scores = block_scores(query_heads, key_heads, start, length)
        weights = jnp.exp(scores - block_total[..., None])
        low_weights = weights.astype(jnp.bfloat16)
        back_block_rows = lax.dynamic_slice_in_dim(back_heads, start, BLOCK, 0)
        back_weights = jnp.einsum(
            "qhd,khd->hqk", back_block_rows, value_heads, preferred_element_type=jnp.float32
        )
        inner = jnp.sum(weights * back_weights, -1, keepdims=True)
        back_scores = (weights * (back_weights - inner)).astype(jnp.bfloat16)
        back_query = jnp.einsum(
            "hqk,khd->qhd", back_scores, key_heads, preferred_element_type=jnp.float32
        )
        key_sum = key_sum + jnp.einsum(
            "hqk,qhd->khd", back_scores, query_block, preferred_element_type=jnp.float32
        )
        value_sum = value_sum + jnp.einsum(
            "hqk,qhd->khd", low_weights, back_block_rows, preferred_element_type=jnp.float32
        )
        return ((key_sum, value_sum), back_query.astype(jnp.bfloat16).reshape(BLOCK, -1))

    starts = jnp.arange(seq_len // BLOCK, dtype=jnp.int32) * BLOCK
    zero_sums = jnp.zeros(key_heads.shape, jnp.float32)
    (key_sum, value_sum), back_queries = lax.scan(
        back_block, (zero_sums, zero_sums), (starts, log_total)
    )
    return (
        back_queries.reshape(seq_len, -1),
        key_sum.astype(jnp.bfloat16).reshape(seq_len, -1),
        value_sum.astype(jnp.bfloat16).reshape(seq_len, -1),
    )


def body(
    hidden,
    lengths,
    first_gain,
    first_shift,
    projection_in,
    query_value_bias,
    projection_out,
    out_bias,
    second_gain,
    second_shift,
    up_weight,
    up_bias,
    down_weight,
    down_bias,
    cotangent,
):
    row_count = hidden.shape[0]
    model_width = hidden.shape[1]
    heads_width = projection_in.shape[2]
    hidden_width = up_weight.shape[1]
    group_rows = row_count * lax.axis_size("mp")
    scale = HEAD_DIM ** (-0.5)
    stream = hidden.astype(jnp.float32)
    first_hat, first_inverse = normalize(stream)
    first_normed = lax.all_gather(
        (first_hat * first_gain + first_shift).astype(jnp.bfloat16), "mp", axis=0, tiled=True
    )
    projection_flat = projection_in.reshape(model_width, 3 * heads_width)
    projected = jnp.dot(first_normed, projection_flat, preferred_element_type=jnp.float32).reshape(
        group_rows, 3, heads_width
    )
    queries = ((projected[:, 0] + query_value_bias[0]) * scale).astype(jnp.bfloat16)
    keys_all = projected[:, 1].astype(jnp.bfloat16)
    values_all = (projected[:, 2] + query_value_bias[1]).astype(jnp.bfloat16)
    member = 0
    context_piece, total_piece = attend(queries, keys_all, values_all, lengths[member])
    total_parts = [total_piece]
    middle = (
        stream
        + lax.psum_scatter(
            jnp.dot(context_piece, projection_out, preferred_element_type=jnp.float32).astype(
                jnp.bfloat16
            ),
            "mp",
            scatter_dimension=0,
            tiled=True,
        ).astype(jnp.float32)
        + out_bias
    )
    second_hat, second_inverse = normalize(middle)
    second_local = (second_hat * second_gain + second_shift).astype(jnp.bfloat16)
    second_normed = lax.all_gather(second_local, "mp", axis=0, tiled=True)
    before = jnp.dot(second_normed, up_weight, preferred_element_type=jnp.float32) + up_bias
    activated_full, gelu_back = jax.vjp(exact_gelu, before)
    activated = activated_full.astype(jnp.bfloat16)
    output = (
        middle
        + lax.psum_scatter(
            jnp.dot(activated, down_weight, preferred_element_type=jnp.float32).astype(
                jnp.bfloat16
            ),
            "mp",
            scatter_dimension=0,
            tiled=True,
        ).astype(jnp.float32)
        + down_bias
    ).astype(jnp.bfloat16)
    cotangent_rows = lax.all_gather(cotangent, "mp", axis=0, tiled=True)
    down_grad = over_rows(activated, cotangent_rows)
    back_before = gelu_back(over_cols(cotangent_rows, down_weight))[0].astype(jnp.bfloat16)
    up_bias_local = jnp.sum(back_before, 0, dtype=jnp.float32)
    up_bias_whole_grad = lax.dynamic_update_slice_in_dim(
        jnp.zeros((hidden_width * lax.axis_size("mp"),), jnp.float32),
        up_bias_local,
        lax.axis_index("mp") * hidden_width,
        0,
    )
    up_grad = over_rows(second_normed, back_before)
    back_second = lax.psum_scatter(
        over_cols(back_before, up_weight).astype(jnp.bfloat16),
        "mp",
        scatter_dimension=0,
        tiled=True,
    ).astype(jnp.float32)
    out_grad = cotangent.astype(jnp.float32)
    second_gain_grad = jnp.sum(back_second * second_hat, 0)
    second_shift_grad = jnp.sum(back_second, 0)
    back_middle = out_grad + norm_back(back_second, second_hat, second_inverse, second_gain)
    middle_rows = lax.all_gather(back_middle.astype(jnp.bfloat16), "mp", axis=0, tiled=True)
    out_grad_weight = over_rows(context_piece, middle_rows)
    back_context = over_cols(middle_rows, projection_out).astype(jnp.bfloat16)
    member = 0
    query_piece, key_piece, value_piece = attend_back(
        queries, keys_all, values_all, back_context, total_parts[member], lengths[member]
    )
    back_queries = query_piece * scale
    back_projected = jnp.stack([back_queries, key_piece, value_piece], 1).reshape(
        group_rows, 3 * heads_width
    )
    projection_grad = over_rows(first_normed, back_projected).reshape(model_width, 3, heads_width)
    bias_local = jnp.stack(
        [jnp.sum(back_queries, 0, dtype=jnp.float32), jnp.sum(value_piece, 0, dtype=jnp.float32)], 0
    )
    bias_whole = lax.dynamic_update_slice_in_dim(
        jnp.zeros((2, model_width), jnp.float32), bias_local, lax.axis_index("mp") * heads_width, 1
    )
    back_first = lax.psum_scatter(
        over_cols(back_projected, projection_flat).astype(jnp.bfloat16),
        "mp",
        scatter_dimension=0,
        tiled=True,
    ).astype(jnp.float32)
    first_gain_grad = jnp.sum(back_first * first_hat, 0)
    first_shift_grad = jnp.sum(back_first, 0)
    hidden_grad = (
        back_middle + norm_back(back_first, first_hat, first_inverse, first_gain)
    ).astype(jnp.bfloat16)
    projection_grad, out_grad_weight, up_grad, down_grad = (
        lax.psum_scatter(projection_grad, "dp", scatter_dimension=0, tiled=True),
        lax.psum_scatter(out_grad_weight, "dp", scatter_dimension=1, tiled=True),
        lax.psum_scatter(up_grad, "dp", scatter_dimension=0, tiled=True),
        lax.psum_scatter(down_grad, "dp", scatter_dimension=1, tiled=True),
    )
    small_sums = lax.psum(
        (
            first_gain_grad,
            first_shift_grad,
            bias_whole,
            jnp.sum(back_middle, 0),
            second_gain_grad,
            second_shift_grad,
            up_bias_whole_grad,
            jnp.sum(out_grad, 0),
        ),
        ("dp", "mp"),
    )
    return (
        output,
        hidden_grad,
        small_sums[0],
        small_sums[1],
        projection_grad,
        small_sums[2],
        out_grad_weight,
        small_sums[3],
        small_sums[4],
        small_sums[5],
        up_grad,
        small_sums[6],
        down_grad,
        small_sums[7],
    )


def solution(mesh):
    placed = (
        P(("dp", "mp"), None),
        P("dp"),
        P(),
        P(),
        P(None, None, "mp"),
        P(None, "mp"),
        P("mp", None),
        P(),
        P(),
        P(),
        P(None, "mp"),
        P("mp"),
        P("mp", None),
        P(),
        P(("dp", "mp"), None),
    )
    return jax.shard_map(
        body,
        mesh=mesh,
        in_specs=placed,
        out_specs=(
            P(("dp", "mp"), None),
            P(("dp", "mp"), None),
            P(),
            P(),
            P("dp", None, "mp"),
            P(),
            P("mp", "dp"),
            P(),
            P(),
            P(),
            P("dp", "mp"),
            P(),
            P("mp", "dp"),
            P(),
        ),
        check_vma=False,
    )
```

profile of v0, /device:TPU:1, one launch (start us, length us, event | category | flops | bytes accessed | tf_op | source)
XLA Modules:
  0.0 974.1 jit_solution(10461550639862020668)
XLA Ops:
  15.5 62.8 %all-gather.5.cloned.1.call-done = bf16[1536,1024]{1,0:T(8,128)(2,1)} async-done(((bf16[384,1024]{1,0:T(8,128)(2,1)}), bf16[1536,1024]{1,0:T(8,128)(2,1)}) %all-gather.5.cloned.1.call-update) | async-done | bytes 3145744 | tf_op jit(solution)/shard_map/all_gather | solution.py:146
  78.3 5.0 fusion.41
  85.1 85.6 %while.27 = (s32[]{:T(128)}, bf16[3,512,256]{2,1,0:T(8,128)(2,1)}, f32[3,4,512]{2,1,0:T(4,128)S(1)}, s32[3]{0:T(128)S(1)}, s32[]{:T(128)}, /*index=5*/bf16[1536,...) while((s32[]{:T(128)}, bf16[3,512,256]{2,1,0:T(8,128)(2,1)}, ...), condition=%wide.region_5.6_spmd, body=%wide.region_2.5_spmd.sunk | while | flops 832176128 | bytes 44113076 | solution.py:75
  89.5 7.7 select_reduce_fusion.2
  97.2 7.7 exponential_reduce_fusion.2
  105.0 7.7 fusion.123
  117.9 7.7 select_reduce_fusion.2
  125.7 7.7 exponential_reduce_fusion.2
  133.4 7.7 fusion.123
  146.4 7.7 select_reduce_fusion.2
  154.1 7.7 exponential_reduce_fusion.2
  161.9 7.7 fusion.123
  170.6 3.9 convolution_convert_fusion.1
  174.7 58.9 %reduce-scatter.9.cloned.1.call-done = bf16[384,1024]{1,0:T(8,128)(2,1)} async-done(((bf16[1536,1024]{1,0:T(8,128)(2,1)}), bf16[384,1024]{1,0:T(8,128)(2,1)}) %reduce-scatter.9.cloned.1.call-update) | async-done | bytes 786448 | tf_op jit(solution)/shard_map/reduce_scatter | solution.py:161
  239.2 63.2 %all-gather.7.cloned.1.call-done = bf16[1536,1024]{1,0:T(8,128)(2,1)} async-done(((bf16[384,1024]{1,0:T(8,128)(2,1)}), bf16[1536,1024]{1,0:T(8,128)(2,1)}) %all-gather.7.cloned.1.call-update) | async-done | bytes 3145744 | tf_op jit(solution)/shard_map/all_gather | solution.py:173
  302.4 8.6 fusion.73
  311.1 55.0 %all-gather.9.cloned.1.call-done = bf16[1536,1024]{1,0:T(8,128)(2,1)} async-done(((bf16[384,1024]{1,0:T(8,128)(2,1)}), bf16[1536,1024]{1,0:T(8,128)(2,1)}) %all-gather.9.cloned.1.call-update) | async-done | bytes 3145744 | tf_op jit(solution)/shard_map/all_gather | solution.py:189
  366.0 21.4 %convert_reduce_fusion = (f32[1024]{0:T(1024)}, bf16[1536,1024]{1,0:T(8,128)(2,1)S(1)}, f32[1536,1024]{1,0:T(8,128)}) fusion(f32[1536,1024]{1,0:T(8,128)} %fusion.73, f32[1024]{0:T(1024)S(1)} %convert_element_type.116, bf16[1536,1024]{1,0:T(8,128)(2,1)} %all-gather.9.cloned.1.call-done, bf16[1024,1024]{1,0:T(8,128)(2,1)S(1)} %copy-done), kind=kOutput, calls=%fused_computation.50 | convolution fusion | flops 3339189248 | bytes 20979712 | tf_op jit(solution)/shard_map/dot_general | solution.py:36
  389.1 5.0 convolution_convert_fusion.2
  394.2 11.9 %reduce-scatter.11.cloned.1.call-start = ((), (), s32[]{:S(2)}) async-start(), calls=%async_computation.11 | async-start | bytes 3932160 | tf_op jit(solution)/shard_map/reduce_scatter | solution.py:179
  406.1 6.3 multiply_convert_fusion.1
  414.2 4.8 convolution_convert_fusion.3
  419.1 34.0 %reduce-scatter.13.cloned.1.call-done = bf16[384,1024]{1,0:T(8,128)(2,1)} async-done(((bf16[1536,1024]{1,0:T(8,128)(2,1)}), bf16[384,1024]{1,0:T(8,128)(2,1)}) %reduce-scatter.13.cloned.1.call-update) | async-done | bytes 786448 | tf_op jit(solution)/shard_map/reduce_scatter | solution.py:200
  455.7 59.8 %reduce-scatter.11.cloned.1.call-done = bf16[384,1024]{1,0:T(8,128)(2,1)} async-done(((bf16[1536,1024]{1,0:T(8,128)(2,1)}), bf16[384,1024]{1,0:T(8,128)(2,1)}) %reduce-scatter.11.cloned.1.call-update) | async-done | bytes 786448 | tf_op jit(solution)/shard_map/reduce_scatter | solution.py:179
  515.6 4.2 fusion.71
  522.0 63.7 %all-gather.11.cloned.1.call-done = bf16[1536,1024]{1,0:T(8,128)(2,1)} async-done(((bf16[384,1024]{1,0:T(8,128)(2,1)}), bf16[1536,1024]{1,0:T(8,128)(2,1)}) %all-gather.11.cloned.1.call-update) | async-done | bytes 3145744 | tf_op jit(solution)/shard_map/all_gather | solution.py:210
  585.8 3.8 convolution_convert_fusion.4
  589.6 99.7 %while.28 = (s32[]{:T(128)}, f32[1536,4,64]{0,2,1:T(8,128)}, f32[1536,4,64]{0,2,1:T(8,128)}, bf16[3,512,256]{1,2,0:T(8,128)(2,1)}, s32[3]{0:T(128)S(1)}, /*index...) while((s32[]{:T(128)}, f32[1536,4,64]{0,2,1:T(8,128)}, ...), condition=%wide.region_15.16_spmd.clone, body=%wide.region_13.15_spmd.clone.sunk | while | flops 2054291456 | bytes 133234024 | solution.py:111
  597.1 4.2 fusion.136
  601.3 9.2 multiply_reduce_fusion.3
  610.5 6.6 multiply_convert_fusion.4
  630.3 4.2 fusion.136
  634.5 9.2 multiply_reduce_fusion.3
  643.7 6.6 multiply_convert_fusion.4
  663.5 4.2 fusion.136
  667.7 9.2 multiply_reduce_fusion.3
  676.9 6.6 multiply_convert_fusion.4
  700.3 6.3 bitcast_convert_fusion
  706.7 8.2 fusion.76
  715.0 8.3 fusion.75
  724.5 3.9 fusion.74
  733.0 7.0 fusion.39
  742.5 23.1 %reduce-scatter.15.cloned.1.call-done = bf16[384,1024]{1,0:T(8,128)(2,1)} async-done(((bf16[1536,1024]{1,0:T(8,128)(2,1)}), bf16[384,1024]{1,0:T(8,128)(2,1)}) %reduce-scatter.15.cloned.1.call-update) | async-done | bytes 786448 | tf_op jit(solution)/shard_map/reduce_scatter | solution.py:228
  767.6 41.6 %all-reduce = (f32[1024]{0:T(1024)}, f32[1024]{0:T(1024)}, f32[2,1024]{1,0:T(2,128)}, f32[1024]{0:T(1024)}, f32[1024]{0:T(1024)}, /*index=5*/f32[1024]{0:T(1024)}, f32[4096]{0:T(1024)}, f32[1024]{0:T(1024)}) all-reduce(f32[1024]{0:T(1024)S(1)} %get-tuple-element.159, ...), channel_id=1, replica_groups=mesh['dp'=8,'mp'=4] {'dp','mp'}, use_global_device_ids=true, to_apply=%region_20.21 | all-reduce | flops 12288 | bytes 98304 | tf_op jit(solution)/shard_map/psum | solution.py:245
  812.3 9.2 reduce-scatter.23.cloned.1.call-done
  821.5 55.5 %reduce-scatter.21.cloned.1.call-done = f32[128,1024]{1,0:T(8,128)} async-done(((f32[1024,1024]{1,0:T(8,128)}), f32[128,1024]{1,0:T(8,128)}) %reduce-scatter.21.cloned.1.call-update) | async-done | bytes 524304 | tf_op jit(solution)/shard_map/reduce_scatter | solution.py:242
  877.0 39.7 %reduce-scatter.19.cloned.1.call-done = f32[256,128]{1,0:T(8,128)} async-done(((f32[256,1024]{1,0:T(8,128)}), f32[256,128]{1,0:T(8,128)}) %reduce-scatter.19.cloned.1.call-update) | async-done | bytes 131088 | tf_op jit(solution)/shard_map/reduce_scatter | solution.py:241
  916.7 50.2 %reduce-scatter.17.cloned.1.call-done = f32[128,3,256]{2,0,1:T(8,128)} async-done(((f32[1024,3,256]{2,0,1:T(8,128)}), f32[128,3,256]{2,0,1:T(8,128)}) %reduce-scatter.17.cloned.1.call-update) | async-done | bytes 393232 | tf_op jit(solution)/shard_map/reduce_scatter | solution.py:240
  (205 shorter events, 91.6 us)
Async XLA Ops:
  7.2 358.9 %copy-start = (bf16[1024,1024]{1,0:T(8,128)(2,1)S(1)}, bf16[1024,1024]{1,0:T(8,128)(2,1)}, u32[]{:S(2)}) copy-start(bf16[1024,1024]{1,0:T(8,128)(2,1)} %param.31) | copy-start | bytes 6291460
  7.2 5.5 copy-start.33
  7.2 71.1 %all-gather.5.cloned.1.call-start = ((), (), s32[]{:S(2)}) async-start(), calls=%async_computation.8 | async-start | bytes 3932160 | tf_op jit(solution)/shard_map/all_gather | solution.py:146
  8.7 6.8 copy-start.19
  10.2 68.1 %copy-start.23 = (f32[384]{0:T(512)}, f32[384]{0:T(512)S(1)}, u32[]{:S(2)}) copy-start(f32[384]{0:T(512)S(1)} %add_rsqrt_fusion.1) | copy-start | bytes 4612
  12.6 220.9 %reduce-scatter.9.cloned.1.call-start = ((), (), s32[]{:S(2)}) async-start(), calls=%async_computation.9 | async-start | bytes 3932160 | tf_op jit(solution)/shard_map/reduce_scatter | solution.py:161
  174.6 59.0 %copy-start.18 = (f32[1024]{0:T(1024)S(1)}, f32[1024]{0:T(1024)}, u32[]{:S(2)}) copy-start(f32[1024]{0:T(1024)} %param.26) | copy-start | bytes 12292
  174.6 62.6 %copy-start.22 = (f32[1024]{0:T(1024)S(1)}, f32[1024]{0:T(1024)}, u32[]{:S(2)}) copy-start(f32[1024]{0:T(1024)} %param.27) | copy-start | bytes 12292
  174.6 62.6 %copy-start.29 = (f32[1024]{0:T(1024)S(1)}, f32[1024]{0:T(1024)}, u32[]{:S(2)}) copy-start(f32[1024]{0:T(1024)} %param.28) | copy-start | bytes 12292
  174.6 127.8 %all-gather.7.cloned.1.call-start = ((), (), s32[]{:S(2)}) async-start(), calls=%async_computation.10 | async-start | bytes 3932160 | tf_op jit(solution)/shard_map/all_gather | solution.py:173
  233.5 3.7 copy-start.2
  233.5 3.7 copy-start.10
  235.4 3.9 copy-start.32
  238.6 127.4 %all-gather.9.cloned.1.call-start = ((), (), s32[]{:S(2)}) async-start(), calls=%async_computation.12 | async-start | bytes 3932160 | tf_op jit(solution)/shard_map/all_gather | solution.py:189
  239.2 213.9 %reduce-scatter.13.cloned.1.call-start = ((), (), s32[]{:S(2)}) async-start(), calls=%async_computation.13 | async-start | bytes 3932160 | tf_op jit(solution)/shard_map/reduce_scatter | solution.py:200
  366.0 23.1 %copy-start.34 = (bf16[1024,1024]{1,0:T(8,128)(2,1)S(1)}, bf16[1024,1024]{1,0:T(8,128)(2,1)}, u32[]{:S(2)}) copy-start(bf16[1024,1024]{1,0:T(8,128)(2,1)} %param.29) | copy-start | bytes 6291460
  394.2 121.4 %reduce-scatter.11.cloned.1.call-start = ((), (), s32[]{:S(2)}) async-start(), calls=%async_computation.11 | async-start | bytes 3932160 | tf_op jit(solution)/shard_map/reduce_scatter | solution.py:179
  419.0 34.1 %copy-start.3 = (bf16[384,1024]{1,0:T(8,128)(2,1)S(1)}, bf16[384,1024]{1,0:T(8,128)(2,1)}, u32[]{:S(2)}) copy-start(bf16[384,1024]{1,0:T(8,128)(2,1)} %param.19) | copy-start | bytes 2359300
  419.0 34.1 %copy-start.11 = (bf16[384,1024]{1,0:T(8,128)(2,1)S(1)}, bf16[384,1024]{1,0:T(8,128)(2,1)}, u32[]{:S(2)}) copy-start(bf16[384,1024]{1,0:T(8,128)(2,1)} %reduce-scatter.9.cloned.1.call-done) | copy-start | bytes 2359300
  419.0 96.6 %copy-start.31 = (f32[1024]{0:T(1024)S(1)}, f32[1024]{0:T(1024)}, u32[]{:S(2)}) copy-start(f32[1024]{0:T(1024)} %param.32) | copy-start | bytes 12292
  419.0 166.8 %all-gather.11.cloned.1.call-start = ((), (), s32[]{:S(2)}) async-start(), calls=%async_computation.14 | async-start | bytes 3932160 | tf_op jit(solution)/shard_map/all_gather | solution.py:210
  519.7 66.0 %copy-start.17 = (bf16[256,1024]{1,0:T(8,128)(2,1)S(1)}, bf16[256,1024]{1,0:T(8,128)(2,1)}, u32[]{:S(2)}) copy-start(bf16[256,1024]{1,0:T(8,128)(2,1)} %param.25) | copy-start | bytes 1572868
  522.0 243.6 %reduce-scatter.15.cloned.1.call-start = ((), (), s32[]{:S(2)}) async-start(), calls=%async_computation.15 | async-start | bytes 3932160 | tf_op jit(solution)/shard_map/reduce_scatter | solution.py:228
  594.0 3.0 copy-start.7
  601.3 9.2 copy-start.8
  617.1 2.0 copy-start.5
  627.2 3.0 copy-start.7
  634.5 9.2 copy-start.8
  650.3 2.0 copy-start.5
  660.4 3.0 copy-start.7
  667.6 9.2 copy-start.8
  683.5 2.0 copy-start.5
  689.3 8.6 copy-start.9
  693.2 7.1 copy-start.13
  700.3 6.4 copy-start.14
  706.7 114.9 %reduce-scatter.23.cloned.1.call-start = ((), (), s32[]{:S(2)}) async-start(), calls=%async_computation.19 | async-start | bytes 4718592 | tf_op jit(solution)/shard_map/reduce_scatter | solution.py:243
  715.0 162.0 %reduce-scatter.21.cloned.1.call-start = ((), (), s32[]{:S(2)}) async-start(), calls=%async_computation.18 | async-start | bytes 4718592 | tf_op jit(solution)/shard_map/reduce_scatter | solution.py:242
  723.4 193.3 %reduce-scatter.19.cloned.1.call-start = ((), (), s32[]{:S(2)}) async-start(), calls=%async_computation.17 | async-start | bytes 1179648 | tf_op jit(solution)/shard_map/reduce_scatter | solution.py:241
  728.4 238.5 %reduce-scatter.17.cloned.1.call-start = ((), (), s32[]{:S(2)}) async-start(), calls=%async_computation.16 | async-start | bytes 3538944 | tf_op jit(solution)/shard_map/reduce_scatter | solution.py:240
  740.0 25.6 %copy-start.4 = (bf16[384,1024]{1,0:T(8,128)(2,1)S(1)}, bf16[384,1024]{1,0:T(8,128)(2,1)}, u32[]{:S(2)}) copy-start(bf16[384,1024]{1,0:T(8,128)(2,1)} %param.19) | copy-start | bytes 2359300
  740.0 25.6 %copy-start.20 = (f32[384]{0:T(512)S(1)}, f32[384]{0:T(512)}, u32[]{:S(2)}) copy-start(f32[384]{0:T(512)} %copy-done.19) | copy-start | bytes 4612
  740.0 25.6 %copy-start.21 = (f32[1024]{0:T(1024)S(1)}, f32[1024]{0:T(1024)}, u32[]{:S(2)}) copy-start(f32[1024]{0:T(1024)} %param.21) | copy-start | bytes 12292
  740.0 25.6 %copy-start.24 = (f32[384]{0:T(512)S(1)}, f32[384]{0:T(512)}, u32[]{:S(2)}) copy-start(f32[384]{0:T(512)} %copy-done.23) | copy-start | bytes 4612
  740.0 27.5 %copy-start.25 = (f32[1024]{0:T(1024)S(1)}, f32[1024]{0:T(1024)}, u32[]{:S(2)}) copy-start(f32[1024]{0:T(1024)} %get-tuple-element.157) | copy-start | bytes 12292
  740.0 27.5 %copy-start.26 = (f32[1024]{0:T(1024)S(1)}, f32[1024]{0:T(1024)}, u32[]{:S(2)}) copy-start(f32[1024]{0:T(1024)} %get-tuple-element.163) | copy-start | bytes 12292
  740.0 27.5 %copy-start.27 = (f32[1024]{0:T(1024)S(1)}, f32[1024]{0:T(1024)}, u32[]{:S(2)}) copy-start(f32[1024]{0:T(1024)} %get-tuple-element.218) | copy-start | bytes 12292
  740.0 27.5 %copy-start.28 = (f32[1024]{0:T(1024)S(1)}, f32[1024]{0:T(1024)}, u32[]{:S(2)}) copy-start(f32[1024]{0:T(1024)} %get-tuple-element.229) | copy-start | bytes 12292
  740.8 226.0 %copy-start.1 = (bf16[1024,1024]{1,0:T(8,128)(2,1)S(1)}, bf16[1024,1024]{1,0:T(8,128)(2,1)}, u32[]{:S(2)}) copy-start(bf16[1024,1024]{1,0:T(8,128)(2,1)} %param.31) | copy-start | bytes 6291460
  (8 other events, 10.2 us)
Sparse Core Ops, SparseCore 0:
  12.8 65.5 all-gather.4
  174.7 58.7 reduce-scatter.8
  238.7 63.6 all-gather.6
  303.8 62.1 all-gather.8
  394.3 58.7 reduce-scatter.12
  455.3 60.2 reduce-scatter.10
  522.1 63.6 all-gather.10
  706.8 58.7 reduce-scatter.14
  769.5 51.9 reduce-scatter.22
  825.7 51.2 reduce-scatter.20
  880.7 35.8 reduce-scatter.18
  920.5 46.3 reduce-scatter.16
where the time goes:
time: 986 us; the launch traced here: 974 us
  waiting for transfers between devices  576 us (58%)
  matrix products  195 us (20%)
  other arithmetic  94.4 us (10%)
  blocking collectives  41.6 us (4%)
  local copies, waits for them, and re-layouts  27.4 us (3%)
  between operations  15 us (2%)
  loops' own time  12.5 us (1%)
  starting transfers between devices  12.4 us (1%)
    all_gather x1, waiting for transfers between devices, body(): lax.all_gather(back_middle.astype(jnp.bfloat16), 'mp', axis=0, tiled=True)  63.7 us
    all_gather x1, waiting for transfers between devices, body(): second_normed = lax.all_gather(second_local, 'mp', axis=0, tiled=True)  63.2 us
    all_gather x1, waiting for transfers between devices, body(): lax.all_gather((first_hat * first_gain + first_shift).astype(jnp.bfloat16...  62.8 us
    reduce_scatter x1, waiting for transfers between devices, body(): lax.psum_scatter(jnp.dot(activated, down_weight, preferred_element_type=j...  59.8 us
    reduce_scatter x1, waiting for transfers between devices, body(): lax.psum_scatter(jnp.dot(context_piece, projection_out, preferred_element...  58.9 us
    reduce_scatter x1, waiting for transfers between devices, body(): lax.psum_scatter(up_grad, 'dp', scatter_dimension=0, tiled=True)  55.5 us
    all_gather x1, waiting for transfers between devices, body(): cotangent_rows = lax.all_gather(cotangent, 'mp', axis=0, tiled=True)  55 us
    reduce_scatter x1, waiting for transfers between devices, body(): lax.psum_scatter(projection_grad, 'dp', scatter_dimension=0, tiled=True)  50.2 us
  transfers between devices with their start and end apart: 12, of which 12 were waited for; matrix products, arithmetic and copies ran while one was open for 7% of the time, Pallas kernels for 0%

commit v1 on v0

v1 whole, which is shorter than its diff:
```python
import jax
import jax.numpy as jnp
from jax import lax
from jax.experimental import pallas as pl
from jax.experimental.pallas import tpu as pltpu
from jax.sharding import PartitionSpec as P

HEAD_DIM = 64
TILE = 256
NEGATIVE = -1e30

def mm(left, right):
    return jnp.dot(left, right, preferred_element_type=jnp.float32)

def split_three(value):
    high = value.astype(jnp.bfloat16)
    rest = value - high.astype(jnp.float32)
    low = rest.astype(jnp.bfloat16)
    return high, low, (rest - low.astype(jnp.float32)).astype(jnp.bfloat16)

def forward_kernel(length_ref, q_ref, k_ref, v_ref, context_ref, total_ref, q_turned, v_turned, keys_at, out_turned):
    rows, width = q_ref.shape
    heads = width // HEAD_DIM
    length = length_ref[0]
    q_turned[...] = q_ref[...].T
    v_turned[...] = v_ref[...].T
    key_row = lax.broadcasted_iota(jnp.int32, (rows, width), 0)
    lane = lax.broadcasted_iota(jnp.int32, (rows, width), 1)
    feature = lax.broadcasted_iota(jnp.int32, (width, TILE), 0)
    key_at = lax.broadcasted_iota(jnp.int32, (TILE, TILE), 0)
    query_at = lax.broadcasted_iota(jnp.int32, (TILE, TILE), 1)

    def one_head(head, _):
        first = pl.multiple_of(head * HEAD_DIM, HEAD_DIM)
        spare = lax.rem(head + 1, heads) * HEAD_DIM
        off = jnp.where(key_row < length, 0.0, NEGATIVE).astype(jnp.bfloat16)
        keys_at[...] = jnp.where(lane == spare, off, k_ref[...])
        for tile in range(rows // TILE):
            cols = slice(tile * TILE, (tile + 1) * TILE)
            count = (tile + 1) * TILE
            query = q_turned[:, cols]
            query = jnp.where(feature // HEAD_DIM == head, query, jnp.where(feature == spare, 1.0, 0.0).astype(jnp.bfloat16))
            scores = mm(keys_at[:count, :], query)
            last = jnp.where(key_at <= query_at, scores[tile * TILE :], NEGATIVE)
            highest = jnp.max(last, 0, keepdims=True)
            if tile:
                highest = jnp.maximum(highest, jnp.max(scores[: tile * TILE], 0, keepdims=True))
            weights = jnp.exp(last - highest)
            total = jnp.sum(weights, 0, keepdims=True)
            low = weights.astype(jnp.bfloat16)
            if tile:
                before = jnp.exp(scores[: tile * TILE] - highest)
                total = total + jnp.sum(before, 0, keepdims=True)
                low = jnp.concatenate([before.astype(jnp.bfloat16), low], 0)
            out = mm(v_turned[pl.ds(first, HEAD_DIM), :count], low)
            out_turned[pl.ds(first, HEAD_DIM), cols] = out / total
            total_ref[pl.ds(head, 1), cols] = highest + jnp.log(total)
        return 0

    lax.fori_loop(0, heads, one_head, 0)
    context_ref[...] = out_turned[...].T.astype(jnp.bfloat16)

def attend(queries, keys, values, length):
    rows, width = queries.shape
    whole = lambda: pl.BlockSpec(memory_space=pltpu.VMEM)
    return pl.pallas_call(
        forward_kernel,
        out_shape=(jax.ShapeDtypeStruct((rows, width), jnp.bfloat16), jax.ShapeDtypeStruct((8, rows), jnp.float32)),
        in_specs=[pl.BlockSpec(memory_space=pltpu.SMEM), whole(), whole(), whole()],
        out_specs=(whole(), whole()),
        scratch_shapes=[
            pltpu.VMEM((width, rows), jnp.bfloat16),
            pltpu.VMEM((width, rows), jnp.bfloat16),
            pltpu.VMEM((rows, width), jnp.bfloat16),
            pltpu.VMEM((width, rows), jnp.float32),
        ],
        compiler_params=pltpu.CompilerParams(vmem_limit_bytes=48 << 20),
        cost_estimate=pl.CostEstimate(flops=2 * rows * rows * width * 2, bytes_accessed=8 * rows * width, transcendentals=rows * rows * 2),
        name="attend",
    )(length, queries, keys, values)

def backward_kernel(length_ref, q_ref, k_ref, v_ref, c_ref, g_ref, total_ref, dq_ref, dk_ref, dv_ref,
                    q_turned, k_turned, g_turned, product, q_side, g_side, q_head, g_head, dq_turned, dk_sum, dv_sum):
    rows, width = q_ref.shape
    heads = width // HEAD_DIM
    length = length_ref[0]
    q_turned[...] = q_ref[...].T
    k_turned[...] = k_ref[...].T
    g_turned[...] = g_ref[...].T
    product[...] = (g_ref[...].astype(jnp.float32) * c_ref[...].astype(jnp.float32)).T
    dk_sum[...] = jnp.zeros_like(dk_sum)
    dv_sum[...] = jnp.zeros_like(dv_sum)
    lane_all = lax.broadcasted_iota(jnp.int32, (rows, width), 1)
    feature = lax.broadcasted_iota(jnp.int32, (width, rows), 0)
    lane = lax.broadcasted_iota(jnp.int32, (TILE, width), 1)
    key_at = lax.broadcasted_iota(jnp.int32, (TILE, TILE), 0)
    query_at = lax.broadcasted_iota(jnp.int32, (TILE, TILE), 1)
    none = jnp.zeros((), jnp.bfloat16)

    def one_head(head, _):
        first = pl.multiple_of(head * HEAD_DIM, HEAD_DIM)
        spare = lax.rem(head + 1, heads) * HEAD_DIM
        total = total_ref[pl.ds(head, 1), :]
        inner = jnp.sum(product[pl.ds(first, HEAD_DIM), :], 0, keepdims=True)
        mine = feature // HEAD_DIM == head
        def side(turned, taken, one):
            high, low, least = split_three(-taken)
            extra = jnp.where(feature == spare, high, jnp.where(feature == spare + 1, low, jnp.where(feature == spare + 2, least,
                jnp.where(feature == spare + 3, one, none))))
            return jnp.where(mine, turned, extra)
        q_side[...] = side(q_turned[...], total, jnp.ones((), jnp.bfloat16))
        g_side[...] = side(g_turned[...], inner, none)
        own = lane_all // HEAD_DIM == head
        q_head[...] = jnp.where(own, q_ref[...], none)
        g_head[...] = jnp.where(own, g_ref[...], none)
        for tile in range(rows // TILE):
            at = slice(tile * TILE, (tile + 1) * TILE)
            key_row = lax.broadcasted_iota(jnp.int32, (TILE, width), 0) + tile * TILE
            off = jnp.where(key_row < length, 0.0, NEGATIVE).astype(jnp.bfloat16)
            ones = (lane >= spare) & (lane < spare + 3)
            one = jnp.ones((), jnp.bfloat16)
            keys = jnp.where(ones, one, jnp.where(lane == spare + 3, off, k_ref[at, :]))
            values = jnp.where(ones, one, v_ref[at, :])
            scores = mm(keys, q_side[:, tile * TILE :])
            back = mm(values, g_side[:, tile * TILE :])
            weights = jnp.exp(scores)
            near = jnp.where(key_at <= query_at, weights[:, :TILE], 0.0)
            if tile + 1 < rows // TILE:
                weights = jnp.concatenate([near, weights[:, TILE:]], 1)
            else:
                weights = near
            low = weights.astype(jnp.bfloat16)
            back_scores = (weights * back).astype(jnp.bfloat16)
            dv_sum[at, :] += mm(low, g_head[tile * TILE :, :])
            dk_sum[at, :] += mm(back_scores, q_head[tile * TILE :, :])
            dq = mm(k_turned[pl.ds(first, HEAD_DIM), at], back_scores)
            if tile:
                dq_turned[pl.ds(first, HEAD_DIM), tile * TILE :] += dq
            else:
                dq_turned[pl.ds(first, HEAD_DIM), :] = dq
        return 0

    lax.fori_loop(0, heads, one_head, 0)
    dq_ref[...] = (dq_turned[...].T.astype(jnp.bfloat16).astype(jnp.float32) * HEAD_DIM**-0.5).astype(jnp.bfloat16)
    dk_ref[...] = dk_sum[...].astype(jnp.bfloat16)
    dv_ref[...] = dv_sum[...].astype(jnp.bfloat16)

def attend_back(queries, keys, values, context, back_context, total, length):
    rows, width = queries.shape
    whole = lambda: pl.BlockSpec(memory_space=pltpu.VMEM)
    flat = jax.ShapeDtypeStruct((rows, width), jnp.bfloat16)
    low, wide = jnp.bfloat16, jnp.float32
    return pl.pallas_call(
        backward_kernel,
        out_shape=(flat, flat, flat),
        in_specs=[pl.BlockSpec(memory_space=pltpu.SMEM)] + [whole()] * 6,
        out_specs=(whole(), whole(), whole()),
        scratch_shapes=[
            pltpu.VMEM((width, rows), low), pltpu.VMEM((width, rows), low), pltpu.VMEM((width, rows), low),
            pltpu.VMEM((width, rows), wide), pltpu.VMEM((width, rows), low), pltpu.VMEM((width, rows), low),
            pltpu.VMEM((rows, width), low), pltpu.VMEM((rows, width), low), pltpu.VMEM((width, rows), wide),
            pltpu.VMEM((rows, width), wide), pltpu.VMEM((rows, width), wide),
        ],
        compiler_params=pltpu.CompilerParams(vmem_limit_bytes=56 << 20),
        cost_estimate=pl.CostEstimate(flops=5 * rows * rows * width * 2, bytes_accessed=20 * rows * width, transcendentals=rows * rows * 2),
        name="attend_back",
    )(length, queries, keys, values, context, back_context, total)

EPS = 1e-05


def normalize(values):
    centered = values - jnp.mean(values, -1, keepdims=True)
    inverse = lax.rsqrt(jnp.mean(centered * centered, -1, keepdims=True) + EPS)
    return (centered * inverse, inverse)


def norm_back(incoming, scaled_in, inverse, gain):
    weighted = incoming * gain
    return inverse * (
        weighted
        - jnp.mean(weighted, -1, keepdims=True)
        - scaled_in * jnp.mean(weighted * scaled_in, -1, keepdims=True)
    )


def over_rows(left, right):
    return lax.dot_general(left, right, (((0,), (0,)), ((), ())), preferred_element_type=jnp.float32)


def over_cols(left, right):
    return lax.dot_general(left, right, (((1,), (1,)), ((), ())), preferred_element_type=jnp.float32)


def feed_kernel(core_ref, x_ref, g_ref, up_ref, bias_ref, down_ref, act_ref, back_ref, sums_ref,
                out_own, out_other, x_own, x_other, out_sum, x_sum):
    step = pl.program_id(0)
    rows = x_ref.shape[0]
    half = rows // 2
    up, down = up_ref[0], down_ref[0]
    before = mm(x_ref[...], up) + bias_ref[0]
    inside = 0.5 * (1.0 + lax.erf(before * 0.5**0.5))
    slope = inside + before * (jnp.exp(-0.5 * before * before) * (0.5 / jnp.pi) ** 0.5)
    act = (before * inside).astype(jnp.bfloat16)
    back = (over_cols(g_ref[...], down) * slope).astype(jnp.bfloat16)
    act_ref[...] = act
    back_ref[...] = back
    sums_ref[0] = jnp.sum(back.astype(jnp.float32), 0, keepdims=True)
    out = mm(act, down)
    grad = over_cols(back, up)

    @pl.when(step == 0)
    def _():
        out_sum[...] = out
        x_sum[...] = grad

    @pl.when(step > 0)
    def _():
        out_sum[...] += out
        x_sum[...] += grad

    @pl.when(step == pl.num_programs(0) - 1)
    def _():
        out_own[...] = out_sum[:half, :]
        out_other[...] = out_sum[half:, :].astype(jnp.bfloat16)
        x_own[...] = x_sum[:half, :]
        x_other[...] = x_sum[half:, :].astype(jnp.bfloat16)


def feed(core, x, g, up, bias, down):
    rows, width = x.shape
    shards, _, hidden = up.shape
    part = hidden // 2
    low, wide = jnp.bfloat16, jnp.float32
    once = lambda shape: pl.BlockSpec(shape, lambda t, c: (0, 0))
    flat = lambda kind: jax.ShapeDtypeStruct((rows // 2, width), kind)
    return pl.pallas_call(
        feed_kernel,
        grid_spec=pltpu.PrefetchScalarGridSpec(
            num_scalar_prefetch=1,
            grid=(shards,),
            in_specs=[
                once((rows, width)),
                once((rows, width)),
                pl.BlockSpec((1, width, part), lambda t, c: (t, 0, c[0])),
                pl.BlockSpec((1, 1, part), lambda t, c: (t, 0, c[0])),
                pl.BlockSpec((1, part, width), lambda t, c: (t, c[0], 0)),
            ],
            out_specs=[
                pl.BlockSpec((rows, part), lambda t, c: (0, t)),
                pl.BlockSpec((rows, part), lambda t, c: (0, t)),
                pl.BlockSpec((1, 1, part), lambda t, c: (t, 0, 0)),
            ]
            + [once((rows // 2, width))] * 4,
            scratch_shapes=[pltpu.VMEM((rows, width), wide)] * 2,
        ),
        out_shape=(
            jax.ShapeDtypeStruct((rows, shards * part), low),
            jax.ShapeDtypeStruct((rows, shards * part), low),
            jax.ShapeDtypeStruct((shards, 1, part), wide),
            flat(wide),
            flat(low),
            flat(wide),
            flat(low),
        ),
        compiler_params=pltpu.CompilerParams(vmem_limit_bytes=56 << 20),
        cost_estimate=pl.CostEstimate(flops=8 * rows * width * shards * part, bytes_accessed=4 * shards * width * part, transcendentals=2 * rows * shards * part),
        name="feed",
    )(core, x, g, up, bias, down)


def turn(size, by):
    return [(at, (at + by) % size) for at in range(size)]


def flip(size, bit):
    return [(at, at ^ bit) for at in range(size)]


def add_up(values):
    for axis in ("dp", "mp"):
        bit = 1
        while bit < lax.axis_size(axis):
            values = values + lax.ppermute(values, axis, flip(lax.axis_size(axis), bit))
            bit *= 2
    return values


def body(hidden, lengths, first_gain, first_shift, projection_in, query_value_bias, projection_out, out_bias,
         second_gain, second_shift, up_weight, up_bias, down_weight, down_bias, cotangent):
    rows, width = hidden.shape
    heads_width = projection_in.shape[2]
    hidden_width = up_weight.shape[1]
    groups, members = lax.axis_size("dp"), lax.axis_size("mp")
    group, member = lax.axis_index("dp"), lax.axis_index("mp")
    core = group % 2
    half = hidden_width // 2
    scale = HEAD_DIM ** (-0.5)
    low, wide = jnp.bfloat16, jnp.float32
    both = ("mp", "dp")
    same_core = [list(range(at, groups, 2)) for at in range(2)]
    swap = lambda value: lax.ppermute(value, "dp", flip(groups, 1))
    pass_on = lambda value, by: lax.ppermute(value, "mp", turn(members, by))

    def gathered(weight):
        count = weight.shape[0] // groups
        piece = lax.dynamic_slice_in_dim(weight, group * count, count, 0)
        return lax.all_gather(piece, both, axis=0, tiled=True)

    stream = hidden.astype(wide)
    first_hat, first_inverse = normalize(stream)
    first_own = (first_hat * first_gain + first_shift).astype(low)
    bias_all = lax.all_gather(up_bias, "mp", axis=0, tiled=True).astype(wide).reshape(members, 1, hidden_width)
    out_full = gathered(projection_out)
    up_full = gathered(up_weight).reshape(members, width, hidden_width)
    down_full = gathered(down_weight).reshape(members, hidden_width, width)

    first_full = jnp.zeros((members * rows, width), low)
    held = first_own
    for by in range(members):
        first_full = lax.dynamic_update_slice_in_dim(first_full, held, (member - by) % members * rows, 0)
        if by < members - 1:
            held = pass_on(held, 1)
    weight_flat = projection_in.reshape(width, 3 * heads_width)
    projected = lambda at: jnp.dot(first_full, projection_in[:, at], preferred_element_type=wide)
    queries = ((projected(0) + query_value_bias[0]) * scale).astype(low)
    keys = projected(1).astype(low)
    values = (projected(2) + query_value_bias[1]).astype(low)
    context, total = attend(queries, keys, values, lengths)

    context_rows = jnp.zeros((rows, width), low)
    for by in range(members):
        part = lax.dynamic_slice_in_dim(context, (member + by) % members * rows, rows, 0)
        part = pass_on(part, by) if by else part
        context_rows = lax.dynamic_update_slice_in_dim(context_rows, part, (member - by) % members * heads_width, 1)
    middle = stream + jnp.dot(context_rows, out_full, preferred_element_type=wide) + out_bias
    second_hat, second_inverse = normalize(middle)
    second_own = (second_hat * second_gain + second_shift).astype(low)
    second_pair = jnp.concatenate([second_own, swap(second_own)], 0)
    cotangent_pair = jnp.concatenate([cotangent, swap(cotangent)], 0)
    activated, back_before, up_bias_part, out_own, out_other, back_own, back_other = feed(
        core.reshape(1), second_pair, cotangent_pair, up_full, bias_all, down_full
    )
    back_second = back_own + swap(back_other).astype(wide)
    output = (middle + out_own + swap(out_other).astype(wide) + down_bias).astype(low)
    out_grad = cotangent.astype(wide)
    second_gain_grad = jnp.sum(back_second * second_hat, 0)
    second_shift_grad = jnp.sum(back_second, 0)
    back_middle = out_grad + norm_back(back_second, second_hat, second_inverse, second_gain)
    low_middle = back_middle.astype(low)
    back_rows = over_cols(low_middle, out_full).astype(low)
    back_context = jnp.zeros((members * rows, heads_width), low)
    for by in range(members):
        part = lax.dynamic_slice_in_dim(back_rows, (member + by) % members * heads_width, heads_width, 1)
        part = pass_on(part, by) if by else part
        back_context = lax.dynamic_update_slice_in_dim(back_context, part, (member - by) % members * rows, 0)

    up_part = over_rows(second_pair, back_before).astype(low)
    down_part = over_rows(cotangent_pair, activated).astype(low)
    out_part = over_rows(low_middle, context_rows).astype(low)
    spread = lambda value: lax.psum_scatter(value, "dp", scatter_dimension=0, axis_index_groups=same_core, tiled=True)
    up_part, down_part, out_part = spread(up_part), spread(down_part), spread(out_part)

    def summed(chunk):
        held = chunk((member - 1) % members).astype(low)
        for by in range(2, members + 1):
            held = pass_on(held, 1).astype(wide) + chunk((member - by) % members)
            held = held.astype(low) if by < members else held
        return held

    def weight_chunk(at):
        return jnp.concatenate(
            [lax.dynamic_slice_in_dim(part, at * wide_of, wide_of, 1) for part, wide_of in ((up_part, half), (down_part, half), (out_part, heads_width))], 1
        ).astype(wide)

    weight_sum = summed(weight_chunk)
    count = width // groups
    kept = lax.dynamic_slice_in_dim(weight_sum, core * count, count, 0)
    given = lax.dynamic_slice_in_dim(weight_sum, (1 - core) * count, count, 0).astype(low)
    taken = swap(given).astype(wide)
    first_kept = core == 0
    ordered = lambda at: jnp.concatenate(
        [jnp.where(first_kept, kept[:, at], taken[:, at]), jnp.where(first_kept, taken[:, at], kept[:, at])], 1
    )
    up_grad = ordered(slice(0, half))
    down_grad = ordered(slice(half, 2 * half)).T
    out_weight_grad = (kept[:, 2 * half :] + taken[:, 2 * half :]).T

    back_queries, back_keys, back_values = attend_back(queries, keys, values, context, back_context, total, lengths)
    back_projected = jnp.concatenate([back_queries, back_keys, back_values], 1)
    projection_part = over_rows(first_full, back_projected)
    projection_grad = lax.psum_scatter(projection_part.astype(low), "dp", scatter_dimension=0, tiled=True)
    projection_grad = projection_grad.astype(wide).reshape(-1, 3, heads_width)
    weight_wide = weight_flat.astype(wide)
    projected_sums = jnp.sum(back_projected, 0, dtype=wide)
    first_shift_grad = jnp.sum(weight_wide * projected_sums, 1)
    first_gain_grad = (jnp.sum(weight_wide * projection_part, 1) - first_shift * first_shift_grad) / first_gain
    back_first = summed(
        lambda at: over_cols(lax.dynamic_slice_in_dim(back_projected, at * rows, rows, 0), weight_flat)
    )
    hidden_grad = (back_middle + norm_back(back_first, first_hat, first_inverse, first_gain)).astype(low)

    placed = lambda value, size, at: lax.dynamic_update_slice(jnp.zeros((size,), wide), value, (at,))
    up_bias_sums = jnp.zeros((members, 2, half), wide)
    up_bias_sums = lax.dynamic_update_slice(up_bias_sums, up_bias_part, (0, core, 0)).reshape(-1)
    sums = [
        first_gain_grad,
        first_shift_grad,
        placed(projected_sums[:heads_width], width, member * heads_width),
        placed(projected_sums[2 * heads_width :], width, member * heads_width),
        jnp.sum(back_middle, 0),
        second_gain_grad,
        second_shift_grad,
        jnp.sum(out_grad, 0),
        up_bias_sums,
    ]
    sums = add_up(jnp.concatenate(sums).reshape(-1, 128)).reshape(-1)
    small = [sums[at * width : (at + 1) * width] for at in range(8)]
    return (
        output,
        hidden_grad,
        small[0],
        small[1],
        projection_grad,
        jnp.stack([small[2], small[3]]),
        out_weight_grad,
        small[4],
        small[5],
        small[6],
        up_grad,
        sums[8 * width :],
        down_grad,
        small[7],
    )


def solution(mesh):
    placed = (
        P(("dp", "mp"), None),
        P("dp"),
        P(),
        P(),
        P(None, None, "mp"),
        P(None, "mp"),
        P("mp", None),
        P(),
        P(),
        P(),
        P(None, "mp"),
        P("mp"),
        P("mp", None),
        P(),
        P(("dp", "mp"), None),
    )
    return jax.shard_map(
        body,
        mesh=mesh,
        in_specs=placed,
        out_specs=(
            P(("dp", "mp"), None),
            P(("dp", "mp"), None),
            P(),
            P(),
            P("dp", None, "mp"),
            P(),
            P("mp", "dp"),
            P(),
            P(),
            P(),
            P("dp", "mp"),
            P(),
            P("mp", "dp"),
            P(),
        ),
        check_vma=False,
    )
```

time: 986 us -> 554 us (0.56)
  waiting for transfers between devices: 576 us -> 307 us
  matrix products: 195 us -> 48.9 us
  other arithmetic: 94.4 us -> 27.1 us
  Pallas kernels: 0 us -> 59.2 us
  blocking collectives: 41.6 us -> 13 us
  starting transfers between devices: 12.4 us -> 31.8 us
  local copies, waits for them, and re-layouts: 27.4 us -> 42.1 us
  loops' own time: 12.5 us -> 0 us
    reduce_scatter x8 -> x3, waiting for transfers between devices: 330 us -> 56 us  [body(): lax.psum_scatter(value, 'dp', scatter_dimension=0, axis_index_groups=same...]
    ppermute x0 -> x25, waiting for transfers between devices: none -> 158 us  [the longest x15 125 us: body(): pass_on = lambda value, by: lax.ppermute(value, 'mp', turn(members, by))]
    all_gather x4 -> x3, waiting for transfers between devices: 245 us -> 93.7 us  [gathered(): return lax.all_gather(piece, both, axis=0, tiled=True)]
    dot_general x25 -> x4, matrix products: 131 us -> 12.1 us  [the longest x3 9.18 us: body(): jnp.dot(first_full, projection_in[:, at], preferred_element_type=wide)]
    pallas_call x0 -> x3, Pallas kernels: none -> 59.2 us  [the longest x1 22.2 us: feed(): pl.pallas_call(feed_kernel, grid_spec=pltpu.PrefetchScalarGridSpec(num_sc...]
    psum x1 -> x0, blocking collectives: 41.6 us -> none  [body(): lax.psum((first_gain_grad, first_shift_grad, bias_whole, jnp.sum(back_mid...]
    convert_element_type x11 -> x5, other arithmetic: 37.9 us -> 5.53 us  [the longest x2 3.73 us: summed(): held = held.astype(low) if by < members else held]
    ppermute x0 -> x25, starting transfers between devices: none -> 31.5 us  [the longest x15 20.9 us: body(): pass_on = lambda value, by: lax.ppermute(value, 'mp', turn(members, by))]
  transfers between devices with their start and end apart: 12 -> 32, of which waited for: 12 -> 18; matrix products, arithmetic and copies ran while one was open for 7% -> 18% of each run, Pallas kernels for 0% -> 7%
where the time goes in v1:
time: 554 us; the launch traced here: 545 us
  waiting for transfers between devices  307 us (55%)
  Pallas kernels  59.2 us (11%)
  matrix products  48.9 us (9%)
  local copies, waits for them, and re-layouts  42.1 us (8%)
  starting transfers between devices  31.8 us (6%)
  other arithmetic  27.1 us (5%)
  between operations  15.8 us (3%)
  blocking collectives  13 us (2%)
    ppermute x15, waiting for transfers between devices, body(): pass_on = lambda value, by: lax.ppermute(value, 'mp', turn(members, by))  125 us
    all_gather x3, waiting for transfers between devices, gathered(): return lax.all_gather(piece, both, axis=0, tiled=True)  93.7 us
    reduce_scatter x3, waiting for transfers between devices, body(): lax.psum_scatter(value, 'dp', scatter_dimension=0, axis_index_groups=same...  56 us
    ppermute x5, waiting for transfers between devices, add_up(): values = values + lax.ppermute(values, axis, flip(lax.axis_size(axis), bit))  30.2 us
    dot_general x4, matrix products, over_rows(): lax.dot_general(left, right, (((0,), (0,)), ((), ())), preferred_element_...  23.1 us
    pallas_call x1, Pallas kernels, feed(): pl.pallas_call(feed_kernel, grid_spec=pltpu.PrefetchScalarGridSpec(num_sc...  22.2 us
    pallas_call x1, Pallas kernels, attend_back(): pl.pallas_call(backward_kernel, out_shape=(flat, flat, flat), in_specs=[p...  21.4 us
    ppermute x15, starting transfers between devices, body(): pass_on = lambda value, by: lax.ppermute(value, 'mp', turn(members, by))  20.9 us
  transfers between devices with their start and end apart: 32, of which 18 were waited for; matrix products, arithmetic and copies ran while one was open for 18% of the time, Pallas kernels for 7%

profile of v1, /device:TPU:1, one launch (start us, length us, event | category | flops | bytes accessed | tf_op | source)
XLA Modules:
  0.0 545.3 jit_solution(13526513795257326991)
XLA Ops:
  12.1 2.1 broadcast_in_dim.9
  15.5 2.2 collective-permute-start
  17.8 20.6 %collective-permute-done = bf16[384,1024]{1,0:T(8,128)(2,1)S(1)} collective-permute-done((bf16[384,1024]{1,0:T(8,128)(2,1)S(1)}, bf16[384,1024]{1,0:T(8,128)(2,1)S(1)}, u32[]{:S(2)}, u32[]{:S(2)}) %collective-permute-start) | collective-permute-done | bytes 786464 | tf_op jit(solution)/shard_map/ppermute | solution.py:303
  38.3 22.4 %collective-permute-done.1 = bf16[384,1024]{1,0:T(8,128)(2,1)S(1)} collective-permute-done((bf16[384,1024]{1,0:T(8,128)(2,1)S(1)}, bf16[384,1024]{1,0:T(8,128)(2,1)S(1)}, u32[]{:S(2)}, u32[]{:S(2)}) %collective-permute-start.1) | collective-permute-done | bytes 786464 | tf_op jit(solution)/shard_map/ppermute | solution.py:303
  63.4 21.8 %collective-permute-done.2 = bf16[384,1024]{1,0:T(8,128)(2,1)S(1)} collective-permute-done((bf16[384,1024]{1,0:T(8,128)(2,1)S(1)}, bf16[384,1024]{1,0:T(8,128)(2,1)S(1)}, u32[]{:S(2)}, u32[]{:S(2)}) %collective-permute-start.2) | collective-permute-done | bytes 786464 | tf_op jit(solution)/shard_map/ppermute | solution.py:303
  86.2 2.9 convolution_convert_fusion.2.k_ref
  89.1 3.2 fusion.2.v_ref
  92.3 3.2 fusion.1.q_ref
  95.5 15.7 %attend.1 = (bf16[1536,256]{1,0:T(8,128)(2,1)S(1)}, f32[8,1536]{1,0:T(8,128)S(1)}) custom-call(s32[1]{0:T(128)S(6)} %copy.66.length_ref, bf16[1536,256]{1,0:T(8,128)(2,1)S(1)} %fusion.1.q_ref, bf16[1536,256]{1,0:T(8,128)(2,1)S(1)} %convolution_convert_fusion.2.k_ref, bf16[1536,256]{1,0:T(8,128)(2,1)S(1)} %fusion.2.v_ref), custom_call_target="tpu_custom_call" | custom-call | flops 2415919104 | bytes 3145728 | tf_op jit(solution)/shard_map/attend/pallas_call | solution.py:66
  112.1 3.1 collective-permute-start.7
  115.2 3.4 collective-permute-start.5
  118.7 12.8 %collective-permute-done.4 = bf16[384,256]{1,0:T(8,128)(2,1)S(1)} collective-permute-done((bf16[384,256]{1,0:T(8,128)(2,1)S(1)}, bf16[384,256]{1,0:T(8,128)(2,1)S(1)}, u32[]{:S(2)}, u32[]{:S(2)}) %collective-permute-start.4) | collective-permute-done | bytes 196640 | tf_op jit(solution)/shard_map/ppermute | solution.py:303
  131.5 6.3 %collective-permute-done.5 = bf16[384,256]{1,0:T(8,128)(2,1)S(1)} collective-permute-done((bf16[384,256]{1,0:T(8,128)(2,1)S(1)}, bf16[384,256]{1,0:T(8,128)(2,1)S(1)}, u32[]{:S(2)}, u32[]{:S(2)}) %collective-permute-start.5) | collective-permute-done | bytes 196640 | tf_op jit(solution)/shard_map/ppermute | solution.py:303
  137.9 2.9 fusion.49
  142.8 13.0 %all_gather.14 = bf16[4096]{0:T(1024)(128)(2,1)S(1)} all-gather(bf16[1024]{0:T(1024)(128)(2,1)S(1)} %copy-done.51), channel_id=1, replica_groups=mesh['dp'=8,'mp'=4] {'mp'}, dimensions={0}, use_global_device_ids=true | all-gather | bytes 10240 | tf_op jit(solution)/shard_map/all_gather | solution.py:313
  156.3 2.1 constant_dynamic-update-slice_fusion.1
  158.5 2.1 constant_dynamic-update-slice_fusion.g_ref
  162.0 14.1 %all-gather.6.cloned.1.call-done = bf16[4096,1024]{1,0:T(8,128)(2,1)} async-done(((bf16[128,1024]{1,0:T(8,128)(2,1)}), bf16[4096,1024]{1,0:T(8,128)(2,1)}) %all-gather.6.cloned.1.call-update) | async-done | bytes 8388624 | tf_op jit(solution)/shard_map/all_gather | solution.py:308
  176.1 79.6 %all-gather.8.cloned.1.call-done = bf16[4096,1024]{1,0:T(8,128)(2,1)} async-done(((bf16[128,1024]{1,0:T(8,128)(2,1)}), bf16[4096,1024]{1,0:T(8,128)(2,1)}) %all-gather.8.cloned.1.call-update) | async-done | bytes 8388624 | tf_op jit(solution)/shard_map/all_gather | solution.py:308
  255.7 22.2 %feed.1 = (bf16[768,2048]{1,0:T(8,128)(2,1)}, bf16[768,2048]{1,0:T(8,128)(2,1)}, f32[4,1,512]{2,1,0:T(1,128)}, f32[384,1024]{1,0:T(8,128)}, bf16[384,1024]{1,0:T...) custom-call(s32[1]{0:T(128)} %bitcast.5.core_ref, bf16[768,1024]{1,0:T(8,128)(2,1)} %pad_maximum_fusion.x_ref, ...), custom_call_target="tpu_custom_call" | custom-call | flops 12884901888 | bytes 8388608 | tf_op jit(solution)/shard_map/feed/pallas_call | solution.py:237
  278.4 2.0 collective-permute-done.9
  280.4 3.0 multiply_reduce_fusion.2
  283.4 3.8 fusion.45
  287.2 2.8 convolution_convert_fusion.3
  291.3 7.0 %convolution_convert_fusion.1 = bf16[1024,2048]{1,0:T(8,128)(2,1)} fusion(bf16[768,2048]{1,0:T(8,128)(2,1)} %get-tuple-element.36, bf16[384,1024]{1,0:T(8,128)(2,1)S(1)} %copy-done.28, bf16[384,1024]{1,0:T(8,128)(2,1)S(1)} %copy-done.15), kind=kOutput, calls=%fused_computation.2 | convolution fusion | flops 3226468352 | bytes 8912896 | tf_op jit(solution)/shard_map/dot_general | solution.py:188
  298.3 8.0 %convolution_convert_fusion = bf16[1024,2048]{1,0:T(8,128)(2,1)} fusion(bf16[768,1024]{1,0:T(8,128)(2,1)} %constant_dynamic-update-slice_fusion.g_ref, bf16[768,2048]{1,0:T(8,128)(2,1)} %get-tuple-element.37), kind=kOutput, calls=%fused_computation.1 | convolution fusion | flops 3223322624 | bytes 8912896 | tf_op jit(solution)/shard_map/dot_general | solution.py:188
  306.4 2.6 convolution_convert_fusion.5
  316.4 10.4 %collective-permute-start.12 = (bf16[384,256]{1,0:T(8,128)(2,1)}, bf16[384,256]{1,0:T(8,128)(2,1)S(1)}, u32[]{:S(2)}, u32[]{:S(2)}) collective-permute-start(bf16[384,256]{1,0:T(8,128)(2,1)} %get-tuple-element.92), channel_id=1, source_target_pairs={{0,3},{1,0},{2,1},{3,2},{4,7},{5,4},{6,5},{7,6},{8,11},{9,8},{10,9... | collective-permute-start | bytes 589832 | tf_op jit(solution)/shard_map/ppermute | solution.py:303
  328.8 3.0 collective-permute-done.12
  332.5 21.4 %attend_back.1 = (bf16[1536,256]{1,0:T(8,128)(2,1)}, bf16[1536,256]{1,0:T(8,128)(2,1)}, bf16[1536,256]{1,0:T(8,128)(2,1)}) custom-call(s32[1]{0:T(128)S(6)} %copy.66.length_ref, bf16[1536,256]{1,0:T(8,128)(2,1)} %copy-done.5, bf16[1536,256]{1,0:T(8,128)(2,1)} %copy-done.3, bf16[1536,256]{1,0:T(8,128)(2,1)} %copy-done.4, bf16[1536,256]{1,0:T(8,128)(2,1)} %copy-done.2, ...), custom_call_target="tpu_custom_call" | custom-call | flops 6039797760 | bytes 7864320 | tf_op jit(solution)/shard_map/attend_back/pallas_call | solution.py:153
  353.9 2.2 constant_dynamic-update-slice_fusion.4
  358.3 2.2 convert_reduce_fusion
  361.9 5.4 fusion.47
  368.3 2.7 convolution_convert_fusion.4
  375.8 1.9 constant_dynamic-slice_fusion
  379.3 2.1 constant_dynamic-slice_fusion.2
  381.4 54.4 %reduce-scatter.9.cloned.1.call-done = bf16[256,2048]{1,0:T(8,128)(2,1)} async-done(((bf16[1024,2048]{1,0:T(8,128)(2,1)}), bf16[256,2048]{1,0:T(8,128)(2,1)}) %reduce-scatter.9.cloned.1.call-update) | async-done | bytes 1048592 | tf_op jit(solution)/shard_map/reduce_scatter | solution.py:361
  435.8 2.1 constant_dynamic-slice_fusion.1
  442.3 1.8 collective-permute-done.18
  445.8 3.0 add_convert_fusion.1
  448.9 11.0 %collective-permute-done.19 = f32[96,128]{1,0:T(8,128)S(1)} collective-permute-done((f32[96,128]{1,0:T(8,128)S(1)}, f32[96,128]{1,0:T(8,128)S(1)}, u32[]{:S(2)}, u32[]{:S(2)}) %collective-permute-start.19) | collective-permute-done | bytes 49184 | tf_op jit(solution)/shard_map/ppermute | solution.py:284
  460.5 17.4 %collective-permute-done.20 = f32[96,128]{1,0:T(8,128)} collective-permute-done((f32[96,128]{1,0:T(8,128)}, f32[96,128]{1,0:T(8,128)}, u32[]{:S(2)}, u32[]{:S(2)}) %collective-permute-start.20) | collective-permute-done | bytes 49184 | tf_op jit(solution)/shard_map/ppermute | solution.py:284
  478.7 2.3 add_convert_fusion.5
  481.6 3.0 add_convert_fusion
  487.9 11.0 %collective-permute-done.22 = bf16[256,1280]{1,0:T(8,128)(2,1)} collective-permute-done((bf16[256,1280]{1,0:T(8,128)(2,1)}, bf16[256,1280]{1,0:T(8,128)(2,1)}, u32[]{:S(2)}, u32[]{:S(2)}) %collective-permute-start.22) | collective-permute-done | bytes 655392 | tf_op jit(solution)/shard_map/ppermute | solution.py:303
  500.4 15.4 %collective-permute-done.15 = bf16[384,1024]{1,0:T(8,128)(2,1)} collective-permute-done((bf16[384,1024]{1,0:T(8,128)(2,1)}, bf16[384,1024]{1,0:T(8,128)(2,1)}, u32[]{:S(2)}, u32[]{:S(2)}) %collective-permute-start.15) | collective-permute-done | bytes 786464 | tf_op jit(solution)/shard_map/ppermute | solution.py:303
  515.8 2.4 fusion.44
  518.2 11.5 %collective-permute-done.23 = bf16[256,1280]{1,0:T(8,128)(2,1)S(1)} collective-permute-done((bf16[256,1280]{1,0:T(8,128)(2,1)S(1)}, bf16[256,1280]{1,0:T(8,128)(2,1)S(1)}, u32[]{:S(2)}, u32[]{:S(2)}) %collective-permute-start.23) | collective-permute-done | bytes 655392 | tf_op jit(solution)/shard_map/ppermute | solution.py:303
  (234 shorter events, 58.3 us)
Async XLA Ops:
  7.2 130.6 %all-gather.4.cloned.1.call-start = ((), (), s32[]{:S(2)}) async-start(), calls=%async_computation.4 | async-start | bytes 2162688 | tf_op jit(solution)/shard_map/all_gather | solution.py:308
  8.9 167.2 %all-gather.6.cloned.1.call-start = ((), (), s32[]{:S(2)}) async-start(), calls=%async_computation.5 | async-start | bytes 8650752 | tf_op jit(solution)/shard_map/all_gather | solution.py:308
  9.7 245.9 %all-gather.8.cloned.1.call-start = ((), (), s32[]{:S(2)}) async-start(), calls=%async_computation.6 | async-start | bytes 8650752 | tf_op jit(solution)/shard_map/all_gather | solution.py:308
  11.5 364.3 %reduce-scatter.11.cloned.1.call-start = ((), (), s32[]{:S(2)}) async-start(), calls=%async_computation.9 | async-start | bytes 2621440 | tf_op jit(solution)/shard_map/reduce_scatter | solution.py:361
  14.3 47.1 %copy-start.52 = (f32[2,256]{1,0:T(2,128)S(1)}, f32[2,256]{1,0:T(2,128)}, u32[]{:S(2)}) copy-start(f32[2,256]{1,0:T(2,128)} %param.20) | copy-start | bytes 6148
  15.5 22.8 %collective-permute-start = (bf16[384,1024]{1,0:T(8,128)(2,1)S(1)}, bf16[384,1024]{1,0:T(8,128)(2,1)S(1)}, u32[]{:S(2)}, u32[]{:S(2)}) collective-permute-start(bf16[384,1024]{1,0:T(8,128)(2,1)S(1)} %get-tuple-element.75), channel_id=1, source_target_pairs={{0,1},{1,2},{2,3},{3,0},{4,5},{5,6},{6,7},{7,4},{8,9},{9,10},{10,1... | collective-permute-start | bytes 2359304 | tf_op jit(solution)/shard_map/ppermute | solution.py:303
  38.3 22.4 %collective-permute-start.1 = (bf16[384,1024]{1,0:T(8,128)(2,1)S(1)}, bf16[384,1024]{1,0:T(8,128)(2,1)S(1)}, u32[]{:S(2)}, u32[]{:S(2)}) collective-permute-start(bf16[384,1024]{1,0:T(8,128)(2,1)S(1)} %collective-permute-done), channel_id=1, source_target_pairs={{0,1},{1,2},{2,3},{3,0},{4,5},{5,6},{6,7},{7,4},{8,9},{9,10},{10,1... | collective-permute-start | bytes 2359304 | tf_op jit(solution)/shard_map/ppermute | solution.py:303
  60.7 24.5 %collective-permute-start.2 = (bf16[384,1024]{1,0:T(8,128)(2,1)S(1)}, bf16[384,1024]{1,0:T(8,128)(2,1)S(1)}, u32[]{:S(2)}, u32[]{:S(2)}) collective-permute-start(bf16[384,1024]{1,0:T(8,128)(2,1)S(1)} %collective-permute-done.1), channel_id=1, source_target_pairs={{0,1},{1,2},{2,3},{3,0},{4,5},{5,6},{6,7},{7,4},{8,9},{9,10},{10,1... | collective-permute-start | bytes 2359304 | tf_op jit(solution)/shard_map/ppermute | solution.py:303
  62.3 23.9 %copy-start.10 = (bf16[1024,3,256]{2,0,1:T(8,128)(2,1)S(1)}, bf16[1024,3,256]{2,0,1:T(8,128)(2,1)}, u32[]{:S(2)}) copy-start(bf16[1024,3,256]{2,0,1:T(8,128)(2,1)} %param.19) | copy-start | bytes 4718596
  89.1 6.3 %copy-start.3 = (bf16[1536,256]{1,0:T(8,128)(2,1)}, bf16[1536,256]{1,0:T(8,128)(2,1)S(1)}, u32[]{:S(2)}) copy-start(bf16[1536,256]{1,0:T(8,128)(2,1)S(1)} %convolution_convert_fusion.2.k_ref) | copy-start | bytes 2359300
  95.5 15.7 %copy-start.5 = (bf16[1536,256]{1,0:T(8,128)(2,1)}, bf16[1536,256]{1,0:T(8,128)(2,1)S(1)}, u32[]{:S(2)}) copy-start(bf16[1536,256]{1,0:T(8,128)(2,1)S(1)} %fusion.1.q_ref) | copy-start | bytes 2359300
  111.8 19.7 %copy-start.2 = (bf16[1536,256]{1,0:T(8,128)(2,1)}, bf16[1536,256]{1,0:T(8,128)(2,1)S(1)}, u32[]{:S(2)}) copy-start(bf16[1536,256]{1,0:T(8,128)(2,1)S(1)} %get-tuple-element.26.c_ref) | copy-start | bytes 2359300
  111.9 26.0 %copy-start.8 = (bf16[384,1024]{1,0:T(8,128)(2,1)S(1)}, bf16[384,1024]{1,0:T(8,128)(2,1)}, u32[]{:S(2)}) copy-start(bf16[384,1024]{1,0:T(8,128)(2,1)} %param.15) | copy-start | bytes 2359300
  111.9 26.0 %copy-start.53 = (f32[1024]{0:T(1024)S(1)}, f32[1024]{0:T(1024)}, u32[]{:S(2)}) copy-start(f32[1024]{0:T(1024)} %param.22) | copy-start | bytes 12292
  112.0 6.7 %collective-permute-start.3 = (bf16[384,256]{1,0:T(8,128)(2,1)S(1)}, bf16[384,256]{1,0:T(8,128)(2,1)S(1)}, u32[]{:S(2)}, u32[]{:S(2)}) collective-permute-start(bf16[384,256]{1,0:T(8,128)(2,1)S(1)} %get-tuple-element.98), channel_id=1, source_target_pairs={{0,1},{1,2},{2,3},{3,0},{4,5},{5,6},{6,7},{7,4},{8,9},{9,10},{10,1... | collective-permute-start | bytes 589832 | tf_op jit(solution)/shard_map/ppermute | solution.py:303
  112.0 19.4 %collective-permute-start.4 = (bf16[384,256]{1,0:T(8,128)(2,1)S(1)}, bf16[384,256]{1,0:T(8,128)(2,1)S(1)}, u32[]{:S(2)}, u32[]{:S(2)}) collective-permute-start(bf16[384,256]{1,0:T(8,128)(2,1)S(1)} %get-tuple-element.97), channel_id=1, source_target_pairs={{0,2},{1,3},{2,0},{3,1},{4,6},{5,7},{6,4},{7,5},{8,10},{9,11},{10,... | collective-permute-start | bytes 589832 | tf_op jit(solution)/shard_map/ppermute | solution.py:303
  112.1 46.4 %collective-permute-start.7 = (bf16[384,1024]{1,0:T(8,128)(2,1)}, bf16[384,1024]{1,0:T(8,128)(2,1)}, u32[]{:S(2)}, u32[]{:S(2)}) collective-permute-start(bf16[384,1024]{1,0:T(8,128)(2,1)} %param.29), channel_id=1, source_target_pairs={{0,4},{4,0},{8,12},{12,8},{16,20},{20,16},{24,28},{28,24},{1,5},{5... | collective-permute-start | bytes 2359304 | tf_op jit(solution)/shard_map/ppermute | solution.py:302
  115.2 22.6 %collective-permute-start.5 = (bf16[384,256]{1,0:T(8,128)(2,1)S(1)}, bf16[384,256]{1,0:T(8,128)(2,1)S(1)}, u32[]{:S(2)}, u32[]{:S(2)}) collective-permute-start(bf16[384,256]{1,0:T(8,128)(2,1)S(1)} %get-tuple-element.96), channel_id=1, source_target_pairs={{0,3},{1,0},{2,1},{3,2},{4,7},{5,4},{6,5},{7,6},{8,11},{9,8},{10,9... | collective-permute-start | bytes 589832 | tf_op jit(solution)/shard_map/ppermute | solution.py:303
  141.8 18.7 %copy-start.14 = (bf16[384,1024]{1,0:T(8,128)(2,1)}, bf16[384,1024]{1,0:T(8,128)(2,1)S(1)}, u32[]{:S(2)}) copy-start(bf16[384,1024]{1,0:T(8,128)(2,1)S(1)} %add_convert_fusion.3) | copy-start | bytes 2359300
  141.8 18.7 %collective-permute-start.6 = (bf16[384,1024]{1,0:T(8,128)(2,1)S(1)}, bf16[384,1024]{1,0:T(8,128)(2,1)S(1)}, u32[]{:S(2)}, u32[]{:S(2)}) collective-permute-start(bf16[384,1024]{1,0:T(8,128)(2,1)S(1)} %add_convert_fusion.3), channel_id=1, source_target_pairs={{0,4},{4,0},{8,12},{12,8},{16,20},{20,16},{24,28},{28,24},{1,5},{5... | collective-permute-start | bytes 2359304 | tf_op jit(solution)/shard_map/ppermute | solution.py:302
  277.8 2.6 collective-permute-start.9
  278.1 5.2 collective-permute-start.8
  289.9 89.4 %reduce-scatter.7.cloned.1.call-start = ((), (), s32[]{:S(2)}) async-start(), calls=%async_computation.7 | async-start | bytes 5242880 | tf_op jit(solution)/shard_map/reduce_scatter | solution.py:361
  298.3 137.5 %reduce-scatter.9.cloned.1.call-start = ((), (), s32[]{:S(2)}) async-start(), calls=%async_computation.8 | async-start | bytes 5242880 | tf_op jit(solution)/shard_map/reduce_scatter | solution.py:361
  306.3 179.6 %reduce-scatter.13.cloned.1.call-start = ((), (), s32[]{:S(2)}) async-start(), calls=%async_computation.10 | async-start | bytes 1769472
  310.8 16.0 %collective-permute-start.10 = (bf16[384,256]{1,0:T(8,128)(2,1)}, bf16[384,256]{1,0:T(8,128)(2,1)S(1)}, u32[]{:S(2)}, u32[]{:S(2)}) collective-permute-start(bf16[384,256]{1,0:T(8,128)(2,1)} %get-tuple-element.94), channel_id=1, source_target_pairs={{0,1},{1,2},{2,3},{3,0},{4,5},{5,6},{6,7},{7,4},{8,9},{9,10},{10,1... | collective-permute-start | bytes 589832 | tf_op jit(solution)/shard_map/ppermute | solution.py:303
  312.1 16.0 %collective-permute-start.11 = (bf16[384,256]{1,0:T(8,128)(2,1)}, bf16[384,256]{1,0:T(8,128)(2,1)S(1)}, u32[]{:S(2)}, u32[]{:S(2)}) collective-permute-start(bf16[384,256]{1,0:T(8,128)(2,1)} %get-tuple-element.93), channel_id=1, source_target_pairs={{0,2},{1,3},{2,0},{3,1},{4,6},{5,7},{6,4},{7,5},{8,10},{9,11},{10,... | collective-permute-start | bytes 589832 | tf_op jit(solution)/shard_map/ppermute | solution.py:303
  316.4 15.4 %collective-permute-start.12 = (bf16[384,256]{1,0:T(8,128)(2,1)}, bf16[384,256]{1,0:T(8,128)(2,1)S(1)}, u32[]{:S(2)}, u32[]{:S(2)}) collective-permute-start(bf16[384,256]{1,0:T(8,128)(2,1)} %get-tuple-element.92), channel_id=1, source_target_pairs={{0,3},{1,0},{2,1},{3,2},{4,7},{5,4},{6,5},{7,6},{8,11},{9,8},{10,9... | collective-permute-start | bytes 589832 | tf_op jit(solution)/shard_map/ppermute | solution.py:303
  367.6 6.4 %copy-start.30 = (f32[12288]{0:T(1024)}, f32[12288]{0:T(1024)S(1)}, u32[]{:S(2)}) copy-start(f32[12288]{0:T(1024)S(1)} %constant_dynamic-update-slice_fusion.16) | copy-start | bytes 147460
  367.7 6.4 %collective-permute-start.16 = (f32[96,128]{1,0:T(8,128)S(1)}, f32[96,128]{1,0:T(8,128)S(1)}, u32[]{:S(2)}, u32[]{:S(2)}) collective-permute-start(f32[96,128]{1,0:T(8,128)S(1)} %bitcast.67), channel_id=1, source_target_pairs={{0,4},{4,0},{8,12},{12,8},{16,20},{20,16},{24,28},{28,24},{1,5},{5... | collective-permute-start | bytes 147464 | tf_op jit(solution)/shard_map/ppermute | solution.py:284
  372.6 73.2 %collective-permute-start.13 = (bf16[384,1024]{1,0:T(8,128)(2,1)}, bf16[384,1024]{1,0:T(8,128)(2,1)}, u32[]{:S(2)}, u32[]{:S(2)}) collective-permute-start(bf16[384,1024]{1,0:T(8,128)(2,1)} %convolution_convert_fusion.4), channel_id=1, source_target_pairs={{0,1},{1,2},{2,3},{3,0},{4,5},{5,6},{6,7},{7,4},{8,9},{9,10},{10,1... | collective-permute-start | bytes 2359304 | tf_op jit(solution)/shard_map/ppermute | solution.py:303
  374.7 65.6 %collective-permute-start.17 = (f32[96,128]{1,0:T(8,128)}, f32[96,128]{1,0:T(8,128)}, u32[]{:S(2)}, u32[]{:S(2)}) collective-permute-start(f32[96,128]{1,0:T(8,128)} %bitcast_add_fusion), channel_id=1, source_target_pairs={{0,8},{4,12},{8,0},{12,4},{16,24},{20,28},{24,16},{28,20},{1,9},{5... | collective-permute-start | bytes 147464 | tf_op jit(solution)/shard_map/ppermute | solution.py:284
  381.4 64.4 %copy-start.19 = (bf16[1024,3,256]{0,2,1:T(8,128)(2,1)S(1)}, bf16[1024,3,256]{0,2,1:T(8,128)(2,1)}, u32[]{:S(2)}) copy-start(bf16[1024,3,256]{0,2,1:T(8,128)(2,1)} %copy.33) | copy-start | bytes 4718596
  438.9 39.8 %collective-permute-start.21 = (bf16[256,1280]{1,0:T(8,128)(2,1)}, bf16[256,1280]{1,0:T(8,128)(2,1)}, u32[]{:S(2)}, u32[]{:S(2)}) collective-permute-start(bf16[256,1280]{1,0:T(8,128)(2,1)} %pad_maximum_fusion.1), channel_id=1, source_target_pairs={{0,1},{1,2},{2,3},{3,0},{4,5},{5,6},{6,7},{7,4},{8,9},{9,10},{10,1... | collective-permute-start | bytes 1966088 | tf_op jit(solution)/shard_map/ppermute | solution.py:303
  441.1 3.0 collective-permute-start.18
  444.1 15.7 %collective-permute-start.19 = (f32[96,128]{1,0:T(8,128)S(1)}, f32[96,128]{1,0:T(8,128)S(1)}, u32[]{:S(2)}, u32[]{:S(2)}) collective-permute-start(f32[96,128]{1,0:T(8,128)S(1)} %add.348), channel_id=1, source_target_pairs={{0,1},{1,0},{2,3},{3,2},{4,5},{5,4},{6,7},{7,6},{8,9},{9,8},{10,11... | collective-permute-start | bytes 147464 | tf_op jit(solution)/shard_map/ppermute | solution.py:284
  448.8 32.8 %collective-permute-start.14 = (bf16[384,1024]{1,0:T(8,128)(2,1)}, bf16[384,1024]{1,0:T(8,128)(2,1)}, u32[]{:S(2)}, u32[]{:S(2)}) collective-permute-start(bf16[384,1024]{1,0:T(8,128)(2,1)} %add_convert_fusion.1), channel_id=1, source_target_pairs={{0,1},{1,2},{2,3},{3,0},{4,5},{5,6},{6,7},{7,4},{8,9},{9,10},{10,1... | collective-permute-start | bytes 2359304 | tf_op jit(solution)/shard_map/ppermute | solution.py:303
  460.5 17.4 %collective-permute-start.20 = (f32[96,128]{1,0:T(8,128)}, f32[96,128]{1,0:T(8,128)}, u32[]{:S(2)}, u32[]{:S(2)}) collective-permute-start(f32[96,128]{1,0:T(8,128)} %add.349), channel_id=1, source_target_pairs={{0,2},{1,3},{2,0},{3,1},{4,6},{5,7},{6,4},{7,5},{8,10},{9,11},{10,... | collective-permute-start | bytes 147464 | tf_op jit(solution)/shard_map/ppermute | solution.py:284
  481.0 17.9 %collective-permute-start.22 = (bf16[256,1280]{1,0:T(8,128)(2,1)}, bf16[256,1280]{1,0:T(8,128)(2,1)}, u32[]{:S(2)}, u32[]{:S(2)}) collective-permute-start(bf16[256,1280]{1,0:T(8,128)(2,1)} %add_convert_fusion.5), channel_id=1, source_target_pairs={{0,1},{1,2},{2,3},{3,0},{4,5},{5,6},{6,7},{7,4},{8,9},{9,10},{10,1... | collective-permute-start | bytes 1966088 | tf_op jit(solution)/shard_map/ppermute | solution.py:303
  484.6 31.2 %copy-start.9 = (bf16[384,1024]{1,0:T(8,128)(2,1)S(1)}, bf16[384,1024]{1,0:T(8,128)(2,1)}, u32[]{:S(2)}) copy-start(bf16[384,1024]{1,0:T(8,128)(2,1)} %param.15) | copy-start | bytes 2359300
  484.6 31.2 %copy-start.37 = (f32[384]{0:T(512)S(1)}, f32[384]{0:T(512)}, u32[]{:S(2)}) copy-start(f32[384]{0:T(512)} %copy-done.36) | copy-start | bytes 4612
  484.6 31.2 %copy-start.39 = (f32[384]{0:T(512)S(1)}, f32[384]{0:T(512)}, u32[]{:S(2)}) copy-start(f32[384]{0:T(512)} %copy-done.38) | copy-start | bytes 4612
  484.6 31.2 %copy-start.44 = (f32[1024]{0:T(1024)S(1)}, f32[1024]{0:T(1024)}, u32[]{:S(2)}) copy-start(f32[1024]{0:T(1024)} %param.17) | copy-start | bytes 12292
  484.6 31.2 %collective-permute-start.15 = (bf16[384,1024]{1,0:T(8,128)(2,1)}, bf16[384,1024]{1,0:T(8,128)(2,1)}, u32[]{:S(2)}, u32[]{:S(2)}) collective-permute-start(bf16[384,1024]{1,0:T(8,128)(2,1)} %add_convert_fusion), channel_id=1, source_target_pairs={{0,1},{1,2},{2,3},{3,0},{4,5},{5,6},{6,7},{7,4},{8,9},{9,10},{10,1... | collective-permute-start | bytes 2359304 | tf_op jit(solution)/shard_map/ppermute | solution.py:303
  487.9 27.9 %copy-start.20 = (bf16[1024,3,256]{0,2,1:T(8,128)(2,1)S(1)}, bf16[1024,3,256]{0,2,1:T(8,128)(2,1)}, u32[]{:S(2)}) copy-start(bf16[1024,3,256]{0,2,1:T(8,128)(2,1)} %copy.33) | copy-start | bytes 4718596
  500.3 29.4 %copy-start.22 = (bf16[256,512]{1,0:T(8,128)(2,1)S(1)}, bf16[256,512]{1,0:T(8,128)(2,1)}, u32[]{:S(2)}) copy-start(bf16[256,512]{1,0:T(8,128)(2,1)} %get-tuple-element.87) | copy-start | bytes 786436
  500.4 29.4 %collective-permute-start.23 = (bf16[256,1280]{1,0:T(8,128)(2,1)S(1)}, bf16[256,1280]{1,0:T(8,128)(2,1)S(1)}, u32[]{:S(2)}, u32[]{:S(2)}) collective-permute-start(bf16[256,1280]{1,0:T(8,128)(2,1)S(1)} %add_convert_fusion.4), channel_id=1, source_target_pairs={{0,1},{1,2},{2,3},{3,0},{4,5},{5,6},{6,7},{7,4},{8,9},{9,10},{10,1... | collective-permute-start | bytes 1966088 | tf_op jit(solution)/shard_map/ppermute | solution.py:303
  529.9 2.8 collective-permute-start.24
  (38 other events, 111.8 us)
Sparse Core Ops, SparseCore 0:
  11.5 78.2 all-gather.3
  93.2 82.8 all-gather.5
  179.5 76.0 all-gather.7
  290.1 33.3 reduce-scatter.10
  326.6 52.6 reduce-scatter.6
  382.1 53.6 reduce-scatter.8
  439.4 38.4 reduce-scatter.12
